TPU v7x, 128 devices: a whole 4x4x4 slice. The times are simulated.
128 devices in a mesh: ep: 8 (over y, core), fs: 16 (over z, x).
Axes of the slice: x: 4, y: 4, z: 4, core: 2. Of those that a mesh axis runs over, the one named last changes fastest.
Arguments:
- grads: bfloat16 [8, 8, 256, 14336], P('ep', None, 'fs'), may hold values from -64 to 64
- counts: int32 [8, 8], replicated, may hold values from 16 to 2047
- weight: bfloat16 [8, 256, 14336], P('ep', 'fs'), may hold values from -3 to 3
- mom: float32 [8, 256, 14336], P('ep', 'fs'), may hold values from -64 to 64
- second: float32 [8, 256, 14336], P('ep', 'fs'), may hold values from 0.1 to 10
- in_weight: float32 [6, 32], replicated, may hold values from -2.5 to 2.5
- in_bias: float32 [32], replicated, may hold values from -3 to 3
- out_weight: float32 [32, 2], replicated, may hold values from -1 to 1
- out_bias: float32 [2], replicated, may hold values from -3 to 3
Outputs:
- new_weight: bfloat16 [8, 256, 14336], P('ep')
- new_mom: float32 [8, 256, 14336], P('ep', 'fs')
- new_second: float32 [8, 256, 14336], P('ep', 'fs')
All inputs are finite; a program needn't handle non-finite values.
Results may differ from a plain program's by a relative error of at most 0.0019.
Values may be sent and summed in bfloat16 or wider, within the bound.
A program may use at most 64 MiB of HBM per device.

v0:
```python
import jax
import jax.numpy as jnp
from jax import lax
from jax.sharding import PartitionSpec as P

MOMENTUM_DECAY = 0.9
SECOND_DECAY = 0.99
NORM_EPS = 1e-06
ROOT_EPS = 1e-08
STEP_SCALE = 0.2
EXP_SCALE = 0.5


def from_everyone(value, axis):
    copies = jnp.broadcast_to(value, (lax.axis_size(axis), *value.shape))
    return lax.all_to_all(copies, axis, split_axis=0, concat_axis=0, tiled=True)


def of_everyone(value, axis):
    return from_everyone(value, axis).sum(axis=0)


def in_one(arrays, axis):
    line, at, done = (jnp.concatenate([a.reshape(-1) for a in arrays]), 0, [])
    so_far = of_everyone(line, axis)
    for a in arrays:
        done.append(so_far[at : at + a.size].reshape(a.shape))
        at += a.size
    return tuple(done)


def learned_step(
    gradient,
    mom_next,
    second_next,
    weight,
    grad_norm,
    mom_norm,
    in_weight,
    in_bias,
    out_weight,
    out_bias,
):
    inv_root = lax.rsqrt(second_next + ROOT_EPS)
    features = jnp.stack(
        [
            gradient / grad_norm,
            mom_next / mom_norm,
            mom_next * inv_root,
            gradient * inv_root,
            weight.astype(jnp.float32),
            jnp.broadcast_to(jnp.log(mom_norm), gradient.shape),
        ]
    )
    hidden = jax.nn.relu(
        jnp.einsum("fh,fab->hab", in_weight, features, precision=lax.Precision.HIGHEST)
        + in_bias[:, None, None]
    )
    outputs = (
        jnp.einsum("hk,hab->kab", out_weight, hidden, precision=lax.Precision.HIGHEST)
        + out_bias[:, None, None]
    )
    update = STEP_SCALE * outputs[0] * jnp.exp(EXP_SCALE * outputs[1])
    return (weight.astype(jnp.float32) - update).astype(jnp.bfloat16)


def add_sources(arrived):
    return jnp.sum(arrived.astype(jnp.float32), axis=0)


def per_device(grads, counts, weight, mom, second, in_weight, in_bias, out_weight, out_bias):
    source = lax.axis_index("ep")
    counts_f = counts.astype(jnp.float32)
    totals = jnp.sum(counts_f, axis=0)
    share_row = lax.dynamic_index_in_dim(counts_f, source, 0, keepdims=False) / totals
    weighted = share_row[None, :, None, None] * grads.astype(jnp.float32)
    outgoing = weighted.astype(jnp.bfloat16)
    gradient = add_sources(lax.all_to_all(outgoing, "ep", split_axis=1, concat_axis=0, tiled=True))[
        0
    ]
    mom_here = mom[0]
    second_here = second[0]
    mom_next = MOMENTUM_DECAY * mom_here + (1.0 - MOMENTUM_DECAY) * gradient
    second_next = SECOND_DECAY * second_here + (1.0 - SECOND_DECAY) * gradient * gradient
    entries = gradient.shape[0] * gradient.shape[1] * lax.axis_size("fs")
    grad_sq, mom_sq = in_one((jnp.sum(gradient * gradient), jnp.sum(mom_next * mom_next)), "fs")
    grad_norm = jnp.sqrt(grad_sq / entries + NORM_EPS)
    mom_norm = jnp.sqrt(mom_sq / entries + NORM_EPS)
    width = gradient.shape[1]

    def block_step(items):
        grad_block, mom_block, second_block, weight_block = items
        return learned_step(
            grad_block,
            mom_block,
            second_block,
            weight_block,
            grad_norm,
            mom_norm,
            in_weight,
            in_bias,
            out_weight,
            out_bias,
        )

    blocks = lax.map(
        block_step,
        (
            gradient.reshape(-1, 2, width),
            mom_next.reshape(-1, 2, width),
            second_next.reshape(-1, 2, width),
            weight[0].reshape(-1, 2, width),
        ),
    )
    updated = blocks.reshape(gradient.shape)
    gathered = lax.all_gather(updated[None], "fs", axis=1, tiled=True)
    return (gathered, mom_next[None], second_next[None])


def solution(mesh):
    in_specs = (
        P("ep", None, "fs", None),
        P(),
        P("ep", "fs", None),
        P("ep", "fs", None),
        P("ep", "fs", None),
        P(),
        P(),
        P(),
        P(),
    )
    out_specs = (P("ep", None, None), P("ep", "fs", None), P("ep", "fs", None))
    return jax.shard_map(
        per_device, mesh=mesh, in_specs=in_specs, out_specs=out_specs, check_vma=False
    )
```

profile of v0, /device:TPU:1, one launch (start us, length us, event | category | flops | bytes accessed | tf_op | source)
XLA Modules:
  0.0 246.2 jit_solution(12678078749305325285)
XLA Ops:
  8.6 4.7 %multiply_convert_fusion = bf16[1,8,16,14336]{3,2,0,1:T(8,128)(2,1)} fusion(bf16[1,8,16,14336]{3,2,1,0:T(8,128)(2,1)} %param.11, f32[8]{0:T(128)S(1)} %bitcast_divide_fusion), kind=kLoop, calls=%fused_computation.22 | loop fusion | flops 5505024 | bytes 7340064 | tf_op jit(solution)/shard_map/convert_element_type | solution.py:77
  13.3 6.1 %all-to-all-start = ((bf16[1,8,16,14336]{3,2,0,1:T(8,128)(2,1)}), bf16[1,8,16,14336]{3,2,0,1:T(8,128)(2,1)}, u32[]{:S(2)}, u32[]{:S(2)}) async-start(bf16[1,8,16,14336]{3,2,0,1:T(8,128)(2,1)} %multiply_convert_fusion), calls=%async_computation | async-start | bytes 7340032 | tf_op jit(solution)/shard_map/all_to_all | solution.py:78
  19.7 42.8 %all-to-all-done = bf16[1,8,16,14336]{3,2,0,1:T(8,128)(2,1)} async-done(((bf16[1,8,16,14336]{3,2,0,1:T(8,128)(2,1)}), bf16[1,8,16,14336]{3,2,0,1:T(8,128)(2,1)}, u32[]{:S(2)}, u32[]{:S(2)}) %all-to-all-start) | async-done | bytes 3670048 | tf_op jit(solution)/shard_map/all_to_all | solution.py:78
  62.5 2.6 %convert_reduce_fusion = f32[16,14336]{1,0:T(8,128)S(1)} fusion(bf16[1,8,16,14336]{3,2,0,1:T(8,128)(2,1)} %all-to-all-done), kind=kLoop, calls=%fused_computation.21 | loop fusion | flops 3440640 | bytes 4587520 | tf_op jit(solution)/shard_map/reduce_sum | solution.py:68
  69.5 7.6 %all-to-all-start.1 = ((f32[16,1,2]{2,1,0:T(1,128)}), f32[16,1,2]{2,1,0:T(1,128)S(1)}, u32[]{:S(2)}, u32[]{:S(2)}) async-start(f32[16,1,2]{2,1,0:T(1,128)} %broadcast_in_dim.18), calls=%async_computation.1 | async-start | bytes 16384 | tf_op jit(solution)/shard_map/all_to_all | solution.py:16
  77.3 2.9 %fusion.10 = (f32[1,16,14336]{2,1,0:T(8,128)}, f32[1,16,14336]{2,1,0:T(8,128)}, f32[1,16,14336]{2,1,0:T(8,128)}, f32[1,16,14336]{2,1,0:T(8,128)S(1)}) fusion(f32[16,14336]{1,0:T(8,128)S(1)} %convert_reduce_fusion, f32[1,16,14336]{2,1,0:T(8,128)} %param.15, f32[1,16,14336]{2,1,0:T(8,128)S(1)} %copy-done), kind=kLoop, calls=%fused_computation.26 | loop fusion | flops 1605632 | bytes 6422528 | tf_op jit(solution)/shard_map/add | solution.py:84
  82.5 4.1 %fusion.9 = (f32[8,2,14336]{2,0,1:T(8,128)S(1)}, f32[8,2,14336]{2,0,1:T(8,128)}, f32[8,2,14336]{2,0,1:T(8,128)}) fusion(f32[8,2,14336]{2,1,0:T(2,128)S(1)} %mul.131, f32[8,2,14336]{2,1,0:T(2,128)} %reshape_squeeze.7, f32[8,2,14336]{2,1,0:T(2,128)S(1)} %mul.126), kind=kLoop, calls=%fused_computation.25 | loop fusion | flops 1146880 | bytes 5505024 | tf_op jit(solution)/shard_map/add | solution.py:84
  88.4 75.6 %while.11 = (s32[]{:T(128)}, bf16[8,2,14336]{2,1,0:T(2,128)(2,1)}, bf16[8,2,14336]{2,1,0:T(2,128)(2,1)S(1)}, f32[8,2,14336]{2,0,1:T(8,128)}, f32[]{:T(128)}, /*i...) while((s32[]{:T(128)}, bf16[8,2,14336]{2,1,0:T(2,128)(2,1)}, ...), condition=%wide.region_6.7_spmd, body=%wide.region_5.6_spmd.sunk | while | flops 90316800 | bytes 11298093 | solution.py:106
  88.7 1.8 dynamic-slice_multiply_fusion.3
  91.6 3.2 %fusion.28 = f32[32,2,14336]{2,0,1:T(8,128)S(1)} fusion(f32[6,2,14336]{2,0,1:T(8,128)S(1)} %stack.4, f32[32]{0:T(128)S(1)} %get-tuple-element.350, f32[6,32]{1,0:T(8,128)S(1)} %get-tuple-element.349), kind=kOutput, calls=%fused_computation.2.clone.1 | convolution fusion | flops 67895296 | bytes 4359040 | tf_op jit(solution)/shard_map/while/body/eval_jaxpr/fh,fab->hab/dot_general | solution.py:56
  94.8 2.1 fusion.29
  98.1 1.8 dynamic-slice_multiply_fusion.3
  101.1 3.2 %fusion.28 = f32[32,2,14336]{2,0,1:T(8,128)S(1)} fusion(f32[6,2,14336]{2,0,1:T(8,128)S(1)} %stack.4, f32[32]{0:T(128)S(1)} %get-tuple-element.350, f32[6,32]{1,0:T(8,128)S(1)} %get-tuple-element.349), kind=kOutput, calls=%fused_computation.2.clone.1 | convolution fusion | flops 67895296 | bytes 4359040 | tf_op jit(solution)/shard_map/while/body/eval_jaxpr/fh,fab->hab/dot_general | solution.py:56
  104.3 2.1 fusion.29
  107.6 1.8 dynamic-slice_multiply_fusion.3
  110.5 3.2 %fusion.28 = f32[32,2,14336]{2,0,1:T(8,128)S(1)} fusion(f32[6,2,14336]{2,0,1:T(8,128)S(1)} %stack.4, f32[32]{0:T(128)S(1)} %get-tuple-element.350, f32[6,32]{1,0:T(8,128)S(1)} %get-tuple-element.349), kind=kOutput, calls=%fused_computation.2.clone.1 | convolution fusion | flops 67895296 | bytes 4359040 | tf_op jit(solution)/shard_map/while/body/eval_jaxpr/fh,fab->hab/dot_general | solution.py:56
  113.7 2.1 fusion.29
  117.0 1.8 dynamic-slice_multiply_fusion.3
  120.0 3.2 %fusion.28 = f32[32,2,14336]{2,0,1:T(8,128)S(1)} fusion(f32[6,2,14336]{2,0,1:T(8,128)S(1)} %stack.4, f32[32]{0:T(128)S(1)} %get-tuple-element.350, f32[6,32]{1,0:T(8,128)S(1)} %get-tuple-element.349), kind=kOutput, calls=%fused_computation.2.clone.1 | convolution fusion | flops 67895296 | bytes 4359040 | tf_op jit(solution)/shard_map/while/body/eval_jaxpr/fh,fab->hab/dot_general | solution.py:56
  123.2 2.1 fusion.29
  126.4 1.8 dynamic-slice_multiply_fusion.3
  129.4 3.2 %fusion.28 = f32[32,2,14336]{2,0,1:T(8,128)S(1)} fusion(f32[6,2,14336]{2,0,1:T(8,128)S(1)} %stack.4, f32[32]{0:T(128)S(1)} %get-tuple-element.350, f32[6,32]{1,0:T(8,128)S(1)} %get-tuple-element.349), kind=kOutput, calls=%fused_computation.2.clone.1 | convolution fusion | flops 67895296 | bytes 4359040 | tf_op jit(solution)/shard_map/while/body/eval_jaxpr/fh,fab->hab/dot_general | solution.py:56
  132.6 2.1 fusion.29
  138.9 3.2 %fusion.28 = f32[32,2,14336]{2,0,1:T(8,128)S(1)} fusion(f32[6,2,14336]{2,0,1:T(8,128)S(1)} %stack.4, f32[32]{0:T(128)S(1)} %get-tuple-element.350, f32[6,32]{1,0:T(8,128)S(1)} %get-tuple-element.349), kind=kOutput, calls=%fused_computation.2.clone.1 | convolution fusion | flops 67895296 | bytes 4359040 | tf_op jit(solution)/shard_map/while/body/eval_jaxpr/fh,fab->hab/dot_general | solution.py:56
  142.1 2.1 fusion.29
  148.3 3.2 %fusion.28 = f32[32,2,14336]{2,0,1:T(8,128)S(1)} fusion(f32[6,2,14336]{2,0,1:T(8,128)S(1)} %stack.4, f32[32]{0:T(128)S(1)} %get-tuple-element.350, f32[6,32]{1,0:T(8,128)S(1)} %get-tuple-element.349), kind=kOutput, calls=%fused_computation.2.clone.1 | convolution fusion | flops 67895296 | bytes 4359040 | tf_op jit(solution)/shard_map/while/body/eval_jaxpr/fh,fab->hab/dot_general | solution.py:56
  151.5 2.1 fusion.29
  157.8 3.2 %fusion.28 = f32[32,2,14336]{2,0,1:T(8,128)S(1)} fusion(f32[6,2,14336]{2,0,1:T(8,128)S(1)} %stack.4, f32[32]{0:T(128)S(1)} %get-tuple-element.350, f32[6,32]{1,0:T(8,128)S(1)} %get-tuple-element.349), kind=kOutput, calls=%fused_computation.2.clone.1 | convolution fusion | flops 67895296 | bytes 4359040 | tf_op jit(solution)/shard_map/while/body/eval_jaxpr/fh,fab->hab/dot_general | solution.py:56
  161.0 2.1 fusion.29
  164.0 2.0 broadcast_in_dim_reshape.3
  166.0 66.5 %all-gather.2.cloned.1.call-done = bf16[1,256,14336]{2,1,0:T(8,128)(2,1)} async-done(((bf16[1,16,14336]{2,1,0:T(8,128)(2,1)}), bf16[1,256,14336]{2,1,0:T(8,128)(2,1)}) %all-gather.2.cloned.1.call-update) | async-done | bytes 7340048 | tf_op jit(solution)/shard_map/all_gather | solution.py:116
  232.5 6.9 %copy.86 = bf16[1,256,14336]{2,1,0:T(8,128)(2,1)} copy(bf16[1,256,14336]{2,1,0:T(8,128)(2,1)} %all-gather.2.cloned.1.call-done) | data formatting | bytes 14680064
  (79 shorter events, 33.1 us)
Async XLA Ops:
  13.2 6.1 %copy-start.1 = (bf16[1,16,14336]{2,1,0:T(8,128)(2,1)S(1)}, bf16[1,16,14336]{2,1,0:T(8,128)(2,1)}, u32[]{:S(2)}) copy-start(bf16[1,16,14336]{2,1,0:T(8,128)(2,1)} %param.13) | copy-start | bytes 1376260
  13.3 49.3 %all-to-all-start = ((bf16[1,8,16,14336]{3,2,0,1:T(8,128)(2,1)}), bf16[1,8,16,14336]{3,2,0,1:T(8,128)(2,1)}, u32[]{:S(2)}, u32[]{:S(2)}) async-start(bf16[1,8,16,14336]{3,2,0,1:T(8,128)(2,1)} %multiply_convert_fusion), calls=%async_computation | async-start | bytes 7340032 | tf_op jit(solution)/shard_map/all_to_all | solution.py:78
  19.3 47.3 %copy-start = (f32[1,16,14336]{2,1,0:T(8,128)S(1)}, f32[1,16,14336]{2,1,0:T(8,128)}, u32[]{:S(2)}) copy-start(f32[1,16,14336]{2,1,0:T(8,128)} %param.14) | copy-start | bytes 2752516
  69.5 17.1 %all-to-all-start.1 = ((f32[16,1,2]{2,1,0:T(1,128)}), f32[16,1,2]{2,1,0:T(1,128)S(1)}, u32[]{:S(2)}, u32[]{:S(2)}) async-start(f32[16,1,2]{2,1,0:T(1,128)} %broadcast_in_dim.18), calls=%async_computation.1 | async-start | bytes 16384 | tf_op jit(solution)/shard_map/all_to_all | solution.py:16
  77.1 155.4 %all-gather.2.cloned.1.call-start = ((), (), s32[]{:S(2)}) async-start(), calls=%async_computation.2 | async-start | bytes 7798784 | tf_op jit(solution)/shard_map/all_gather | solution.py:116
  81.9 6.5 %copy-start.2 = (f32[6,32]{1,0:T(8,128)S(1)}, f32[6,32]{1,0:T(8,128)}, u32[]{:S(2)}) copy-start(f32[6,32]{1,0:T(8,128)} %param.16) | copy-start | bytes 2308
  81.9 6.5 %copy-start.3 = (f32[32,2]{0,1:T(2,128)S(1)}, f32[32,2]{0,1:T(2,128)}, u32[]{:S(2)}) copy-start(f32[32,2]{0,1:T(2,128)} %param.18) | copy-start | bytes 772
  81.9 6.5 %copy-start.4 = (f32[32]{0:T(128)S(1)}, f32[32]{0:T(128)}, u32[]{:S(2)}) copy-start(f32[32]{0:T(128)} %param.17) | copy-start | bytes 388
  81.9 6.5 %copy-start.5 = (f32[2]{0:T(128)S(1)}, f32[2]{0:T(128)}, u32[]{:S(2)}) copy-start(f32[2]{0:T(128)} %param.19) | copy-start | bytes 28
Sparse Core Ops, SparseCore 0:
  166.1 66.3 all-gather.1
where the time goes:
time: 247 us; the launch traced here: 246 us
  waiting for transfers between devices  109 us (44%)
  matrix products  42 us (17%)
  other arithmetic  35.8 us (14%)
  local copies, waits for them, and re-layouts  29.4 us (12%)
  between operations  15.4 us (6%)
  starting transfers between devices  13.9 us (6%)
    all_gather x1, waiting for transfers between devices, per_device(): gathered = lax.all_gather(updated[None], 'fs', axis=1, tiled=True)  66.5 us
    all_to_all x1, waiting for transfers between devices, per_device(): lax.all_to_all(outgoing, 'ep', split_axis=1, concat_axis=0, tiled=True)  42.8 us
    dot_general x8, matrix products, learned_step(): jnp.einsum('fh,fab->hab', in_weight, features, precision=lax.Precision.HI...  25.6 us
    dot_general x8, matrix products, learned_step(): jnp.einsum('hk,hab->kab', out_weight, hidden, precision=lax.Precision.HIG...  16.4 us
    mul x8, other arithmetic, learned_step(): gradient * inv_root  14.7 us
    another operation x8, local copies, waits for them, and re-layouts, learned_step(): jnp.stack([gradient / grad_norm, mom_next / mom_norm, mom_next * inv_root...  8.98 us
    all_to_all x1, starting transfers between devices, from_everyone(): return lax.all_to_all(copies, axis, split_axis=0, concat_axis=0, tiled=True)  7.6 us
    unnamed x13, local copies, waits for them, and re-layouts  6.93 us
  transfers between devices with their start and end apart: 3, of which 2 were waited for; matrix products, arithmetic and copies ran while one was open for 4% of the time, Pallas kernels for 0%

commit v1 on v0

--- a/solution.py
+++ b/solution.py
@@ -9,6 +9,24 @@
 ROOT_EPS = 1e-08
 STEP_SCALE = 0.2
 EXP_SCALE = 0.5
+
+
+def ring_gather(value, axis, dim):
+    ways, here, step = (lax.axis_size(axis), lax.axis_index(axis), value.shape[dim])
+    shape = [n * ways if d == dim else n for d, n in enumerate(value.shape)]
+    full = lax.dynamic_update_slice_in_dim(
+        jnp.zeros(shape, value.dtype), value, here * step, axis=dim
+    )
+    going_up = going_down = value
+    for far in range(1, ways // 2 + 1):
+        going_up = lax.ppermute(going_up, axis, [(d, (d + 1) % ways) for d in range(ways)])
+        full = lax.dynamic_update_slice_in_dim(full, going_up, (here - far) % ways * step, axis=dim)
+        if 2 * far < ways:
+            going_down = lax.ppermute(going_down, axis, [(d, (d - 1) % ways) for d in range(ways)])
+            full = lax.dynamic_update_slice_in_dim(
+                full, going_down, (here + far) % ways * step, axis=dim
+            )
+    return full
 
 
 def from_everyone(value, axis):
@@ -113,7 +131,7 @@
         ),
     )
     updated = blocks.reshape(gradient.shape)
-    gathered = lax.all_gather(updated[None], "fs", axis=1, tiled=True)
+    gathered = ring_gather(updated[None], "fs", 1)
     return (gathered, mom_next[None], second_next[None])
 
 

time: 247 us -> 272 us (1.10)
  the two profiles are of different devices: /device:TPU:1 before, /device:TPU:0 now
where the time goes in v1:
time: 272 us; the launch traced here: 271 us
  waiting for transfers between devices  111 us (41%)
  starting transfers between devices  51.1 us (19%)
  matrix products  42 us (15%)
  other arithmetic  37.7 us (14%)
  local copies, waits for them, and re-layouts  26.2 us (10%)
    ppermute x8, waiting for transfers between devices, ring_gather(): lax.ppermute(going_up, axis, [(d, (d + 1) % ways) for d in range(ways)])  63.9 us
    all_to_all x1, waiting for transfers between devices, per_device(): lax.all_to_all(outgoing, 'ep', split_axis=1, concat_axis=0, tiled=True)  43.5 us
    ppermute x7, starting transfers between devices, ring_gather(): lax.ppermute(going_down, axis, [(d, (d - 1) % ways) for d in range(ways)])  38 us
    dot_general x8, matrix products, learned_step(): jnp.einsum('fh,fab->hab', in_weight, features, precision=lax.Precision.HI...  25.6 us
    mul x8, other arithmetic, learned_step(): gradient * inv_root  16.9 us
    dot_general x8, matrix products, learned_step(): jnp.einsum('hk,hab->kab', out_weight, hidden, precision=lax.Precision.HIG...  16.4 us
    another operation x8, local copies, waits for them, and re-layouts, learned_step(): jnp.stack([gradient / grad_norm, mom_next / mom_norm, mom_next * inv_root...  8.98 us
    all_to_all x1, starting transfers between devices, from_everyone(): return lax.all_to_all(copies, axis, split_axis=0, concat_axis=0, tiled=True)  7.89 us
  transfers between devices with their start and end apart: 17, of which 11 were waited for; matrix products, arithmetic and copies ran while one was open for 2% of the time, Pallas kernels for 0%

profile of v1, /device:TPU:0, one launch (start us, length us, event | category | flops | bytes accessed | tf_op | source)
XLA Modules:
  0.0 271.3 jit_solution(6175109779725905088)
XLA Ops:
  2.0 4.7 %multiply_convert_fusion = bf16[1,8,16,14336]{3,2,0,1:T(8,128)(2,1)} fusion(bf16[1,8,16,14336]{3,2,1,0:T(8,128)(2,1)} %param.11, f32[8]{0:T(128)S(1)} %fusion.15), kind=kLoop, calls=%fused_computation.22 | loop fusion | flops 5505024 | bytes 7340064 | tf_op jit(solution)/shard_map/convert_element_type | solution.py:95
  6.8 4.7 %all-to-all-start = ((bf16[1,8,16,14336]{3,2,0,1:T(8,128)(2,1)}), bf16[1,8,16,14336]{3,2,0,1:T(8,128)(2,1)}, u32[]{:S(2)}, u32[]{:S(2)}) async-start(bf16[1,8,16,14336]{3,2,0,1:T(8,128)(2,1)} %multiply_convert_fusion), calls=%async_computation | async-start | bytes 7340032 | tf_op jit(solution)/shard_map/all_to_all | solution.py:96
  12.1 43.5 %all-to-all-done = bf16[1,8,16,14336]{3,2,0,1:T(8,128)(2,1)} async-done(((bf16[1,8,16,14336]{3,2,0,1:T(8,128)(2,1)}), bf16[1,8,16,14336]{3,2,0,1:T(8,128)(2,1)}, u32[]{:S(2)}, u32[]{:S(2)}) %all-to-all-start) | async-done | bytes 3670048 | tf_op jit(solution)/shard_map/all_to_all | solution.py:96
  60.7 2.9 %fusion.10 = (f32[1,16,14336]{2,1,0:T(8,128)}, f32[1,16,14336]{2,1,0:T(8,128)S(1)}, f32[1,16,14336]{2,1,0:T(8,128)}, f32[1,16,14336]{2,1,0:T(8,128)}) fusion(f32[16,14336]{1,0:T(8,128)S(1)} %convert_reduce_fusion, f32[1,16,14336]{2,1,0:T(8,128)} %param.15, f32[1,16,14336]{2,1,0:T(8,128)S(1)} %copy-done.1), kind=kLoop, calls=%fused_computation.26 | loop fusion | flops 1605632 | bytes 6422528 | tf_op jit(solution)/shard_map/add | solution.py:102
  67.7 7.9 %all-to-all-start.1 = ((f32[16,1,2]{2,1,0:T(1,128)}), f32[16,1,2]{2,1,0:T(1,128)S(1)}, u32[]{:S(2)}, u32[]{:S(2)}) async-start(f32[16,1,2]{2,1,0:T(1,128)} %broadcast_in_dim.22), calls=%async_computation.1 | async-start | bytes 16384 | tf_op jit(solution)/shard_map/all_to_all | solution.py:34
  75.6 3.8 %fusion.9 = (f32[8,2,14336]{2,0,1:T(8,128)}, f32[8,2,14336]{2,0,1:T(8,128)}, f32[8,2,14336]{2,0,1:T(8,128)}) fusion(f32[8,2,14336]{2,1,0:T(2,128)S(1)} %mul.179, f32[8,2,14336]{2,1,0:T(2,128)} %reshape_squeeze.7, f32[8,2,14336]{2,1,0:T(2,128)S(1)} %mul.174), kind=kLoop, calls=%fused_computation.25 | loop fusion | flops 1146880 | bytes 5505024 | tf_op jit(solution)/shard_map/add | solution.py:102
  79.4 3.8 %all-to-all-done.1 = f32[16,1,2]{2,1,0:T(1,128)S(1)} async-done(((f32[16,1,2]{2,1,0:T(1,128)}), f32[16,1,2]{2,1,0:T(1,128)S(1)}, u32[]{:S(2)}, u32[]{:S(2)}) %all-to-all-start.1) | async-done | bytes 160 | tf_op jit(solution)/shard_map/all_to_all | solution.py:34
  85.2 77.8 %while.11 = (s32[]{:T(128)}, bf16[8,2,14336]{2,1,0:T(2,128)(2,1)}, bf16[8,2,14336]{2,1,0:T(2,128)(2,1)S(1)}, f32[8,2,14336]{2,0,1:T(8,128)}, f32[]{:T(128)}, /*i...) while((s32[]{:T(128)}, bf16[8,2,14336]{2,1,0:T(2,128)(2,1)}, ...), condition=%wide.region_6.7_spmd, body=%wide.region_5.6_spmd.sunk | while | flops 90316800 | bytes 11298593 | solution.py:124
  88.7 3.2 %fusion.30 = f32[32,2,14336]{2,0,1:T(8,128)S(1)} fusion(f32[6,2,14336]{2,0,1:T(8,128)S(1)} %stack.4, f32[32]{0:T(128)S(1)} %get-tuple-element.350, f32[6,32]{1,0:T(8,128)S(1)} %get-tuple-element.349), kind=kOutput, calls=%fused_computation.2.clone.1 | convolution fusion | flops 67895296 | bytes 4359040 | tf_op jit(solution)/shard_map/while/body/eval_jaxpr/fh,fab->hab/dot_general | solution.py:74
  98.4 3.2 %fusion.30 = f32[32,2,14336]{2,0,1:T(8,128)S(1)} fusion(f32[6,2,14336]{2,0,1:T(8,128)S(1)} %stack.4, f32[32]{0:T(128)S(1)} %get-tuple-element.350, f32[6,32]{1,0:T(8,128)S(1)} %get-tuple-element.349), kind=kOutput, calls=%fused_computation.2.clone.1 | convolution fusion | flops 67895296 | bytes 4359040 | tf_op jit(solution)/shard_map/while/body/eval_jaxpr/fh,fab->hab/dot_general | solution.py:74
  108.1 3.2 %fusion.30 = f32[32,2,14336]{2,0,1:T(8,128)S(1)} fusion(f32[6,2,14336]{2,0,1:T(8,128)S(1)} %stack.4, f32[32]{0:T(128)S(1)} %get-tuple-element.350, f32[6,32]{1,0:T(8,128)S(1)} %get-tuple-element.349), kind=kOutput, calls=%fused_computation.2.clone.1 | convolution fusion | flops 67895296 | bytes 4359040 | tf_op jit(solution)/shard_map/while/body/eval_jaxpr/fh,fab->hab/dot_general | solution.py:74
  117.8 3.2 %fusion.30 = f32[32,2,14336]{2,0,1:T(8,128)S(1)} fusion(f32[6,2,14336]{2,0,1:T(8,128)S(1)} %stack.4, f32[32]{0:T(128)S(1)} %get-tuple-element.350, f32[6,32]{1,0:T(8,128)S(1)} %get-tuple-element.349), kind=kOutput, calls=%fused_computation.2.clone.1 | convolution fusion | flops 67895296 | bytes 4359040 | tf_op jit(solution)/shard_map/while/body/eval_jaxpr/fh,fab->hab/dot_general | solution.py:74
  127.6 3.2 %fusion.30 = f32[32,2,14336]{2,0,1:T(8,128)S(1)} fusion(f32[6,2,14336]{2,0,1:T(8,128)S(1)} %stack.4, f32[32]{0:T(128)S(1)} %get-tuple-element.350, f32[6,32]{1,0:T(8,128)S(1)} %get-tuple-element.349), kind=kOutput, calls=%fused_computation.2.clone.1 | convolution fusion | flops 67895296 | bytes 4359040 | tf_op jit(solution)/shard_map/while/body/eval_jaxpr/fh,fab->hab/dot_general | solution.py:74
  137.3 3.2 %fusion.30 = f32[32,2,14336]{2,0,1:T(8,128)S(1)} fusion(f32[6,2,14336]{2,0,1:T(8,128)S(1)} %stack.4, f32[32]{0:T(128)S(1)} %get-tuple-element.350, f32[6,32]{1,0:T(8,128)S(1)} %get-tuple-element.349), kind=kOutput, calls=%fused_computation.2.clone.1 | convolution fusion | flops 67895296 | bytes 4359040 | tf_op jit(solution)/shard_map/while/body/eval_jaxpr/fh,fab->hab/dot_general | solution.py:74
  147.0 3.2 %fusion.30 = f32[32,2,14336]{2,0,1:T(8,128)S(1)} fusion(f32[6,2,14336]{2,0,1:T(8,128)S(1)} %stack.4, f32[32]{0:T(128)S(1)} %get-tuple-element.350, f32[6,32]{1,0:T(8,128)S(1)} %get-tuple-element.349), kind=kOutput, calls=%fused_computation.2.clone.1 | convolution fusion | flops 67895296 | bytes 4359040 | tf_op jit(solution)/shard_map/while/body/eval_jaxpr/fh,fab->hab/dot_general | solution.py:74
  156.8 3.2 %fusion.30 = f32[32,2,14336]{2,0,1:T(8,128)S(1)} fusion(f32[6,2,14336]{2,0,1:T(8,128)S(1)} %stack.4, f32[32]{0:T(128)S(1)} %get-tuple-element.350, f32[6,32]{1,0:T(8,128)S(1)} %get-tuple-element.349), kind=kOutput, calls=%fused_computation.2.clone.1 | convolution fusion | flops 67895296 | bytes 4359040 | tf_op jit(solution)/shard_map/while/body/eval_jaxpr/fh,fab->hab/dot_general | solution.py:74
  164.7 4.9 %collective-permute-start.1 = (bf16[1,16,14336]{2,1,0:T(8,128)(2,1)S(1)}, bf16[1,16,14336]{2,1,0:T(8,128)(2,1)S(1)}, u32[]{:S(2)}, u32[]{:S(2)}) collective-permute-start(bf16[1,16,14336]{2,1,0:T(8,128)(2,1)S(1)} %broadcast_in_dim_reshape.3), channel_id=1, source_target_pairs={{0,15},{1,0},{2,1},{3,2},{4,3},{5,4},{6,5},{7,6},{8,7},{9,8},{10,9... | collective-permute-start | bytes 1376264 | tf_op jit(solution)/shard_map/ppermute | solution.py:25
  170.5 7.5 %collective-permute-done = bf16[1,16,14336]{2,1,0:T(8,128)(2,1)S(1)} collective-permute-done((bf16[1,16,14336]{2,1,0:T(8,128)(2,1)S(1)}, bf16[1,16,14336]{2,1,0:T(8,128)(2,1)S(1)}, u32[]{:S(2)}, u32[]{:S(2)}) %collective-permute-start) | collective-permute-done | bytes 458784 | tf_op jit(solution)/shard_map/ppermute | solution.py:22
  178.0 5.3 %collective-permute-start.3 = (bf16[1,16,14336]{2,1,0:T(8,128)(2,1)S(1)}, bf16[1,16,14336]{2,1,0:T(8,128)(2,1)S(1)}, u32[]{:S(2)}, u32[]{:S(2)}) collective-permute-start(bf16[1,16,14336]{2,1,0:T(8,128)(2,1)S(1)} %collective-permute-done.1), channel_id=1, source_target_pairs={{0,15},{1,0},{2,1},{3,2},{4,3},{5,4},{6,5},{7,6},{8,7},{9,8},{10,9... | collective-permute-start | bytes 1376264 | tf_op jit(solution)/shard_map/ppermute | solution.py:25
  183.4 7.4 %collective-permute-done.2 = bf16[1,16,14336]{2,1,0:T(8,128)(2,1)S(1)} collective-permute-done((bf16[1,16,14336]{2,1,0:T(8,128)(2,1)S(1)}, bf16[1,16,14336]{2,1,0:T(8,128)(2,1)S(1)}, u32[]{:S(2)}, u32[]{:S(2)}) %collective-permute-start.2) | collective-permute-done | bytes 458784 | tf_op jit(solution)/shard_map/ppermute | solution.py:22
  190.8 5.3 %collective-permute-start.5 = (bf16[1,16,14336]{2,1,0:T(8,128)(2,1)S(1)}, bf16[1,16,14336]{2,1,0:T(8,128)(2,1)S(1)}, u32[]{:S(2)}, u32[]{:S(2)}) collective-permute-start(bf16[1,16,14336]{2,1,0:T(8,128)(2,1)S(1)} %collective-permute-done.3), channel_id=1, source_target_pairs={{0,15},{1,0},{2,1},{3,2},{4,3},{5,4},{6,5},{7,6},{8,7},{9,8},{10,9... | collective-permute-start | bytes 1376264 | tf_op jit(solution)/shard_map/ppermute | solution.py:25
  196.3 6.6 %collective-permute-done.4 = bf16[1,16,14336]{2,1,0:T(8,128)(2,1)S(1)} collective-permute-done((bf16[1,16,14336]{2,1,0:T(8,128)(2,1)S(1)}, bf16[1,16,14336]{2,1,0:T(8,128)(2,1)S(1)}, u32[]{:S(2)}, u32[]{:S(2)}) %collective-permute-start.4) | collective-permute-done | bytes 458784 | tf_op jit(solution)/shard_map/ppermute | solution.py:22
  202.8 5.3 %collective-permute-start.7 = (bf16[1,16,14336]{2,1,0:T(8,128)(2,1)S(1)}, bf16[1,16,14336]{2,1,0:T(8,128)(2,1)S(1)}, u32[]{:S(2)}, u32[]{:S(2)}) collective-permute-start(bf16[1,16,14336]{2,1,0:T(8,128)(2,1)S(1)} %collective-permute-done.5), channel_id=1, source_target_pairs={{0,15},{1,0},{2,1},{3,2},{4,3},{5,4},{6,5},{7,6},{8,7},{9,8},{10,9... | collective-permute-start | bytes 1376264 | tf_op jit(solution)/shard_map/ppermute | solution.py:25
  208.3 6.4 %collective-permute-done.6 = bf16[1,16,14336]{2,1,0:T(8,128)(2,1)S(1)} collective-permute-done((bf16[1,16,14336]{2,1,0:T(8,128)(2,1)S(1)}, bf16[1,16,14336]{2,1,0:T(8,128)(2,1)S(1)}, u32[]{:S(2)}, u32[]{:S(2)}) %collective-permute-start.6) | collective-permute-done | bytes 458784 | tf_op jit(solution)/shard_map/ppermute | solution.py:22
  214.6 5.5 %collective-permute-start.9 = (bf16[1,16,14336]{2,1,0:T(8,128)(2,1)S(1)}, bf16[1,16,14336]{2,1,0:T(8,128)(2,1)S(1)}, u32[]{:S(2)}, u32[]{:S(2)}) collective-permute-start(bf16[1,16,14336]{2,1,0:T(8,128)(2,1)S(1)} %collective-permute-done.7), channel_id=1, source_target_pairs={{0,15},{1,0},{2,1},{3,2},{4,3},{5,4},{6,5},{7,6},{8,7},{9,8},{10,9... | collective-permute-start | bytes 1376264 | tf_op jit(solution)/shard_map/ppermute | solution.py:25
  220.2 7.2 %collective-permute-done.8 = bf16[1,16,14336]{2,1,0:T(8,128)(2,1)S(1)} collective-permute-done((bf16[1,16,14336]{2,1,0:T(8,128)(2,1)S(1)}, bf16[1,16,14336]{2,1,0:T(8,128)(2,1)S(1)}, u32[]{:S(2)}, u32[]{:S(2)}) %collective-permute-start.8) | collective-permute-done | bytes 458784 | tf_op jit(solution)/shard_map/ppermute | solution.py:22
  227.4 5.7 %collective-permute-start.11 = (bf16[1,16,14336]{2,1,0:T(8,128)(2,1)S(1)}, bf16[1,16,14336]{2,1,0:T(8,128)(2,1)S(1)}, u32[]{:S(2)}, u32[]{:S(2)}) collective-permute-start(bf16[1,16,14336]{2,1,0:T(8,128)(2,1)S(1)} %collective-permute-done.9), channel_id=1, source_target_pairs={{0,15},{1,0},{2,1},{3,2},{4,3},{5,4},{6,5},{7,6},{8,7},{9,8},{10,9... | collective-permute-start | bytes 1376264 | tf_op jit(solution)/shard_map/ppermute | solution.py:25
  233.2 8.1 %collective-permute-done.10 = bf16[1,16,14336]{2,1,0:T(8,128)(2,1)S(1)} collective-permute-done((bf16[1,16,14336]{2,1,0:T(8,128)(2,1)S(1)}, bf16[1,16,14336]{2,1,0:T(8,128)(2,1)S(1)}, u32[]{:S(2)}, u32[]{:S(2)}) %collective-permute-start.10) | collective-permute-done | bytes 458784 | tf_op jit(solution)/shard_map/ppermute | solution.py:22
  241.6 5.8 %collective-permute-start.13 = (bf16[1,16,14336]{2,1,0:T(8,128)(2,1)S(1)}, bf16[1,16,14336]{2,1,0:T(8,128)(2,1)S(1)}, u32[]{:S(2)}, u32[]{:S(2)}) collective-permute-start(bf16[1,16,14336]{2,1,0:T(8,128)(2,1)S(1)} %collective-permute-done.11), channel_id=1, source_target_pairs={{0,15},{1,0},{2,1},{3,2},{4,3},{5,4},{6,5},{7,6},{8,7},{9,8},{10,9... | collective-permute-start | bytes 1376264 | tf_op jit(solution)/shard_map/ppermute | solution.py:25
  247.4 9.0 %collective-permute-done.12 = bf16[1,16,14336]{2,1,0:T(8,128)(2,1)S(1)} collective-permute-done((bf16[1,16,14336]{2,1,0:T(8,128)(2,1)S(1)}, bf16[1,16,14336]{2,1,0:T(8,128)(2,1)S(1)}, u32[]{:S(2)}, u32[]{:S(2)}) %collective-permute-start.12) | collective-permute-done | bytes 458784 | tf_op jit(solution)/shard_map/ppermute | solution.py:22
  256.5 11.7 %collective-permute-done.14 = bf16[1,16,14336]{2,1,0:T(8,128)(2,1)S(1)} collective-permute-done((bf16[1,16,14336]{2,1,0:T(8,128)(2,1)S(1)}, bf16[1,16,14336]{2,1,0:T(8,128)(2,1)S(1)}, u32[]{:S(2)}, u32[]{:S(2)}) %collective-permute-start.14) | collective-permute-done | bytes 458784 | tf_op jit(solution)/shard_map/ppermute | solution.py:22
  268.3 3.0 %copy-done = bf16[1,256,14336]{2,1,0:T(8,128)(2,1)} copy-done((bf16[1,256,14336]{2,1,0:T(8,128)(2,1)}, bf16[1,256,14336]{2,1,0:T(8,128)(2,1)S(1)}, u32[]{:S(2)}) %copy-start) | copy-done | bytes 7340056
  (124 shorter events, 66.7 us)
Async XLA Ops:
  2.0 9.7 %copy-start.2 = (bf16[1,16,14336]{2,1,0:T(8,128)(2,1)S(1)}, bf16[1,16,14336]{2,1,0:T(8,128)(2,1)}, u32[]{:S(2)}) copy-start(bf16[1,16,14336]{2,1,0:T(8,128)(2,1)} %param.13) | copy-start | bytes 1376260
  6.8 52.9 %copy-start.1 = (f32[1,16,14336]{2,1,0:T(8,128)S(1)}, f32[1,16,14336]{2,1,0:T(8,128)}, u32[]{:S(2)}) copy-start(f32[1,16,14336]{2,1,0:T(8,128)} %param.14) | copy-start | bytes 2752516
  6.8 48.8 %all-to-all-start = ((bf16[1,8,16,14336]{3,2,0,1:T(8,128)(2,1)}), bf16[1,8,16,14336]{3,2,0,1:T(8,128)(2,1)}, u32[]{:S(2)}, u32[]{:S(2)}) async-start(bf16[1,8,16,14336]{3,2,0,1:T(8,128)(2,1)} %multiply_convert_fusion), calls=%async_computation | async-start | bytes 7340032 | tf_op jit(solution)/shard_map/all_to_all | solution.py:96
  60.6 24.5 %copy-start.3 = (f32[6,32]{1,0:T(8,128)S(1)}, f32[6,32]{1,0:T(8,128)}, u32[]{:S(2)}) copy-start(f32[6,32]{1,0:T(8,128)} %param.16) | copy-start | bytes 2308
  60.7 24.5 %copy-start.4 = (f32[32,2]{0,1:T(2,128)S(1)}, f32[32,2]{0,1:T(2,128)}, u32[]{:S(2)}) copy-start(f32[32,2]{0,1:T(2,128)} %param.18) | copy-start | bytes 772
  60.7 24.5 %copy-start.5 = (f32[32]{0:T(128)S(1)}, f32[32]{0:T(128)}, u32[]{:S(2)}) copy-start(f32[32]{0:T(128)} %param.17) | copy-start | bytes 388
  60.7 24.5 %copy-start.6 = (f32[2]{0:T(128)S(1)}, f32[2]{0:T(128)}, u32[]{:S(2)}) copy-start(f32[2]{0:T(128)} %param.19) | copy-start | bytes 28
  67.7 15.5 %all-to-all-start.1 = ((f32[16,1,2]{2,1,0:T(1,128)}), f32[16,1,2]{2,1,0:T(1,128)S(1)}, u32[]{:S(2)}, u32[]{:S(2)}) async-start(f32[16,1,2]{2,1,0:T(1,128)} %broadcast_in_dim.22), calls=%async_computation.1 | async-start | bytes 16384 | tf_op jit(solution)/shard_map/all_to_all | solution.py:34
  164.2 13.8 %collective-permute-start = (bf16[1,16,14336]{2,1,0:T(8,128)(2,1)S(1)}, bf16[1,16,14336]{2,1,0:T(8,128)(2,1)S(1)}, u32[]{:S(2)}, u32[]{:S(2)}) collective-permute-start(bf16[1,16,14336]{2,1,0:T(8,128)(2,1)S(1)} %broadcast_in_dim_reshape.3), channel_id=1, source_target_pairs={{0,1},{1,2},{2,3},{3,4},{4,5},{5,6},{6,7},{7,8},{8,9},{9,10},{10,1... | collective-permute-start | bytes 1376264 | tf_op jit(solution)/shard_map/ppermute | solution.py:22
  164.7 13.3 %collective-permute-start.1 = (bf16[1,16,14336]{2,1,0:T(8,128)(2,1)S(1)}, bf16[1,16,14336]{2,1,0:T(8,128)(2,1)S(1)}, u32[]{:S(2)}, u32[]{:S(2)}) collective-permute-start(bf16[1,16,14336]{2,1,0:T(8,128)(2,1)S(1)} %broadcast_in_dim_reshape.3), channel_id=1, source_target_pairs={{0,15},{1,0},{2,1},{3,2},{4,3},{5,4},{6,5},{7,6},{8,7},{9,8},{10,9... | collective-permute-start | bytes 1376264 | tf_op jit(solution)/shard_map/ppermute | solution.py:25
  178.0 12.9 %collective-permute-start.2 = (bf16[1,16,14336]{2,1,0:T(8,128)(2,1)S(1)}, bf16[1,16,14336]{2,1,0:T(8,128)(2,1)S(1)}, u32[]{:S(2)}, u32[]{:S(2)}) collective-permute-start(bf16[1,16,14336]{2,1,0:T(8,128)(2,1)S(1)} %collective-permute-done), channel_id=1, source_target_pairs={{0,1},{1,2},{2,3},{3,4},{4,5},{5,6},{6,7},{7,8},{8,9},{9,10},{10,1... | collective-permute-start | bytes 1376264 | tf_op jit(solution)/shard_map/ppermute | solution.py:22
  178.0 12.9 %collective-permute-start.3 = (bf16[1,16,14336]{2,1,0:T(8,128)(2,1)S(1)}, bf16[1,16,14336]{2,1,0:T(8,128)(2,1)S(1)}, u32[]{:S(2)}, u32[]{:S(2)}) collective-permute-start(bf16[1,16,14336]{2,1,0:T(8,128)(2,1)S(1)} %collective-permute-done.1), channel_id=1, source_target_pairs={{0,15},{1,0},{2,1},{3,2},{4,3},{5,4},{6,5},{7,6},{8,7},{9,8},{10,9... | collective-permute-start | bytes 1376264 | tf_op jit(solution)/shard_map/ppermute | solution.py:25
  190.8 12.0 %collective-permute-start.4 = (bf16[1,16,14336]{2,1,0:T(8,128)(2,1)S(1)}, bf16[1,16,14336]{2,1,0:T(8,128)(2,1)S(1)}, u32[]{:S(2)}, u32[]{:S(2)}) collective-permute-start(bf16[1,16,14336]{2,1,0:T(8,128)(2,1)S(1)} %collective-permute-done.2), channel_id=1, source_target_pairs={{0,1},{1,2},{2,3},{3,4},{4,5},{5,6},{6,7},{7,8},{8,9},{9,10},{10,1... | collective-permute-start | bytes 1376264 | tf_op jit(solution)/shard_map/ppermute | solution.py:22
  190.8 12.0 %collective-permute-start.5 = (bf16[1,16,14336]{2,1,0:T(8,128)(2,1)S(1)}, bf16[1,16,14336]{2,1,0:T(8,128)(2,1)S(1)}, u32[]{:S(2)}, u32[]{:S(2)}) collective-permute-start(bf16[1,16,14336]{2,1,0:T(8,128)(2,1)S(1)} %collective-permute-done.3), channel_id=1, source_target_pairs={{0,15},{1,0},{2,1},{3,2},{4,3},{5,4},{6,5},{7,6},{8,7},{9,8},{10,9... | collective-permute-start | bytes 1376264 | tf_op jit(solution)/shard_map/ppermute | solution.py:25
  202.8 11.8 %collective-permute-start.6 = (bf16[1,16,14336]{2,1,0:T(8,128)(2,1)S(1)}, bf16[1,16,14336]{2,1,0:T(8,128)(2,1)S(1)}, u32[]{:S(2)}, u32[]{:S(2)}) collective-permute-start(bf16[1,16,14336]{2,1,0:T(8,128)(2,1)S(1)} %collective-permute-done.4), channel_id=1, source_target_pairs={{0,1},{1,2},{2,3},{3,4},{4,5},{5,6},{6,7},{7,8},{8,9},{9,10},{10,1... | collective-permute-start | bytes 1376264 | tf_op jit(solution)/shard_map/ppermute | solution.py:22
  202.8 11.8 %collective-permute-start.7 = (bf16[1,16,14336]{2,1,0:T(8,128)(2,1)S(1)}, bf16[1,16,14336]{2,1,0:T(8,128)(2,1)S(1)}, u32[]{:S(2)}, u32[]{:S(2)}) collective-permute-start(bf16[1,16,14336]{2,1,0:T(8,128)(2,1)S(1)} %collective-permute-done.5), channel_id=1, source_target_pairs={{0,15},{1,0},{2,1},{3,2},{4,3},{5,4},{6,5},{7,6},{8,7},{9,8},{10,9... | collective-permute-start | bytes 1376264 | tf_op jit(solution)/shard_map/ppermute | solution.py:25
  214.6 12.8 %collective-permute-start.8 = (bf16[1,16,14336]{2,1,0:T(8,128)(2,1)S(1)}, bf16[1,16,14336]{2,1,0:T(8,128)(2,1)S(1)}, u32[]{:S(2)}, u32[]{:S(2)}) collective-permute-start(bf16[1,16,14336]{2,1,0:T(8,128)(2,1)S(1)} %collective-permute-done.6), channel_id=1, source_target_pairs={{0,1},{1,2},{2,3},{3,4},{4,5},{5,6},{6,7},{7,8},{8,9},{9,10},{10,1... | collective-permute-start | bytes 1376264 | tf_op jit(solution)/shard_map/ppermute | solution.py:22
  214.6 12.8 %collective-permute-start.9 = (bf16[1,16,14336]{2,1,0:T(8,128)(2,1)S(1)}, bf16[1,16,14336]{2,1,0:T(8,128)(2,1)S(1)}, u32[]{:S(2)}, u32[]{:S(2)}) collective-permute-start(bf16[1,16,14336]{2,1,0:T(8,128)(2,1)S(1)} %collective-permute-done.7), channel_id=1, source_target_pairs={{0,15},{1,0},{2,1},{3,2},{4,3},{5,4},{6,5},{7,6},{8,7},{9,8},{10,9... | collective-permute-start | bytes 1376264 | tf_op jit(solution)/shard_map/ppermute | solution.py:25
  227.4 13.9 %collective-permute-start.10 = (bf16[1,16,14336]{2,1,0:T(8,128)(2,1)S(1)}, bf16[1,16,14336]{2,1,0:T(8,128)(2,1)S(1)}, u32[]{:S(2)}, u32[]{:S(2)}) collective-permute-start(bf16[1,16,14336]{2,1,0:T(8,128)(2,1)S(1)} %collective-permute-done.8), channel_id=1, source_target_pairs={{0,1},{1,2},{2,3},{3,4},{4,5},{5,6},{6,7},{7,8},{8,9},{9,10},{10,1... | collective-permute-start | bytes 1376264 | tf_op jit(solution)/shard_map/ppermute | solution.py:22
  227.4 14.1 %collective-permute-start.11 = (bf16[1,16,14336]{2,1,0:T(8,128)(2,1)S(1)}, bf16[1,16,14336]{2,1,0:T(8,128)(2,1)S(1)}, u32[]{:S(2)}, u32[]{:S(2)}) collective-permute-start(bf16[1,16,14336]{2,1,0:T(8,128)(2,1)S(1)} %collective-permute-done.9), channel_id=1, source_target_pairs={{0,15},{1,0},{2,1},{3,2},{4,3},{5,4},{6,5},{7,6},{8,7},{9,8},{10,9... | collective-permute-start | bytes 1376264 | tf_op jit(solution)/shard_map/ppermute | solution.py:25
  241.3 15.1 %collective-permute-start.12 = (bf16[1,16,14336]{2,1,0:T(8,128)(2,1)S(1)}, bf16[1,16,14336]{2,1,0:T(8,128)(2,1)S(1)}, u32[]{:S(2)}, u32[]{:S(2)}) collective-permute-start(bf16[1,16,14336]{2,1,0:T(8,128)(2,1)S(1)} %collective-permute-done.10), channel_id=1, source_target_pairs={{0,1},{1,2},{2,3},{3,4},{4,5},{5,6},{6,7},{7,8},{8,9},{9,10},{10,1... | collective-permute-start | bytes 1376264 | tf_op jit(solution)/shard_map/ppermute | solution.py:22
  241.6 14.9 %collective-permute-start.13 = (bf16[1,16,14336]{2,1,0:T(8,128)(2,1)S(1)}, bf16[1,16,14336]{2,1,0:T(8,128)(2,1)S(1)}, u32[]{:S(2)}, u32[]{:S(2)}) collective-permute-start(bf16[1,16,14336]{2,1,0:T(8,128)(2,1)S(1)} %collective-permute-done.11), channel_id=1, source_target_pairs={{0,15},{1,0},{2,1},{3,2},{4,3},{5,4},{6,5},{7,6},{8,7},{9,8},{10,9... | collective-permute-start | bytes 1376264 | tf_op jit(solution)/shard_map/ppermute | solution.py:25
  256.4 11.8 %collective-permute-start.14 = (bf16[1,16,14336]{2,1,0:T(8,128)(2,1)S(1)}, bf16[1,16,14336]{2,1,0:T(8,128)(2,1)S(1)}, u32[]{:S(2)}, u32[]{:S(2)}) collective-permute-start(bf16[1,16,14336]{2,1,0:T(8,128)(2,1)S(1)} %collective-permute-done.12), channel_id=1, source_target_pairs={{0,1},{1,2},{2,3},{3,4},{4,5},{5,6},{6,7},{7,8},{8,9},{9,10},{10,1... | collective-permute-start | bytes 1376264 | tf_op jit(solution)/shard_map/ppermute | solution.py:22
  268.3 3.1 %copy-start = (bf16[1,256,14336]{2,1,0:T(8,128)(2,1)}, bf16[1,256,14336]{2,1,0:T(8,128)(2,1)S(1)}, u32[]{:S(2)}) copy-start(bf16[1,256,14336]{2,1,0:T(8,128)(2,1)S(1)} %constant_dynamic-update-slice_fusion) | copy-start | bytes 22020100
